TPU v7x, 32 devices: a whole 2x2x4 slice. The times are simulated.
32 devices in a mesh: tm: 16 (over z, x, core), space: 2 (over y).
Axes of the slice: x: 2, y: 2, z: 4, core: 2. Of those that a mesh axis runs over, the one named last changes fastest.
Arguments:
- forcing: float32 [16, 8, 128, 128], P('tm', 'space'), may hold values from -6 to 6
- initial: float32 [8, 128, 128], P('space'), may hold values from -6 to 6
- coupling: float32 [8, 128, 128], P('space'), may hold values from 0.3 to 3
- velocity: float32 [3, 8, 128, 128], P(None, 'space'), may hold values from -0.9 to 0.9
Outputs:
- iterate: float32 [16, 8, 128, 128], P('tm', 'space')
All inputs are finite; a program needn't handle non-finite values.
Results may differ from a plain program's by a relative error of at most 0.0003.
Values sent between devices are 32-bit elements; how exact they have to be, the bound alone decides.
A program may use at most 64 MiB of HBM per device.

v0:
```python
import math

import jax
import jax.numpy as jnp
from jax import lax
from jax.sharding import PartitionSpec as P

ITERS = 2
SWEEPS = 8


wrap_alpha = 0.1


def passed_along(array, axis, by):
    size = lax.axis_size(axis)
    pairs = [(i, i + by) for i in range(size) if 0 <= i + by < size]
    return lax.ppermute(array, axis, pairs)


def with_halo(block, sides, width):
    for axis, dim in sides:
        count = lax.axis_size(axis)
        forward = [(i, i + 1) for i in range(count - 1)]
        backward = [(target, source) for source, target in forward]
        low = lax.ppermute(
            lax.slice_in_dim(block, block.shape[dim] - width, None, axis=dim), axis, forward
        )
        high = lax.ppermute(lax.slice_in_dim(block, 0, width, axis=dim), axis, backward)
        block = jnp.concatenate([low, block, high], axis=dim)
    return block


def coupled(extended, coupling, advect):
    total = (coupling - advect[0]) * extended[..., 2:, 1:-1, 1:-1] + (
        coupling + advect[0]
    ) * extended[..., :-2, 1:-1, 1:-1]
    total = (
        total
        + (coupling - advect[1]) * extended[..., 1:-1, 2:, 1:-1]
        + (coupling + advect[1]) * extended[..., 1:-1, :-2, 1:-1]
    )
    total = (
        total
        + (coupling - advect[2]) * extended[..., 1:-1, 1:-1, 2:]
        + (coupling + advect[2]) * extended[..., 1:-1, 1:-1, :-2]
    )
    return total


def tables(total_steps):
    indices = jnp.arange(total_steps, dtype=jnp.int32)
    products = indices[:, None] * indices[None, :] % total_steps
    angles = products.astype(jnp.float32) * (2.0 * math.pi / total_steps)
    return (jnp.cos(angles), jnp.sin(angles))


def matmul(table, columns):
    return jnp.dot(
        table, columns, preferred_element_type=jnp.float32, precision=lax.Precision.HIGHEST
    )


def jacobi(spectrum, coupling, advect, frequency, total_steps, extend):
    radius = math.exp(math.log(wrap_alpha) / total_steps)
    angles = (frequency * (2.0 * math.pi / total_steps))[:, None, None, None]
    diag_re = 1.0 + 6.0 * coupling - radius * jnp.cos(angles)
    diag_im = radius * jnp.sin(angles) + jnp.zeros_like(diag_re)
    modulus = diag_re * diag_re + diag_im * diag_im
    source_re = spectrum[0]
    source_im = spectrum[1]
    value_re = (source_re * diag_re + source_im * diag_im) / modulus
    value_im = (source_im * diag_re - source_re * diag_im) / modulus
    for sweep in range(SWEEPS):
        extended = extend(jnp.stack([value_re, value_im]))
        summed = coupled(extended, coupling, advect)
        sum_re = source_re + summed[0]
        sum_im = source_im + summed[1]
        value_re = (sum_re * diag_re + sum_im * diag_im) / modulus
        value_im = (sum_im * diag_re - sum_re * diag_im) / modulus
    return jnp.stack([value_re, value_im])


def body(forcing, initial, coupling, velocity):
    local_steps = forcing.shape[0]
    groups = lax.axis_size("tm")
    total_steps = local_steps * groups
    time_index = lax.axis_index("tm")
    advect = coupling[None] * velocity
    cosine, sine_table = tables(total_steps)
    global_steps = (time_index * local_steps + jnp.arange(local_steps, dtype=jnp.int32)).astype(
        jnp.float32
    )
    time_weight = jnp.exp(math.log(wrap_alpha) * global_steps / total_steps)[:, None, None, None]
    iterate = jnp.broadcast_to(initial, forcing.shape)

    def forward(piece):
        columns = piece.reshape(piece.shape[0], -1)
        spec_re = matmul(cosine, columns)
        spec_im = -matmul(sine_table, columns)
        return jnp.stack([spec_re, spec_im]).reshape((2,) + piece.shape)

    for repeat in range(ITERS):
        before = passed_along(iterate[-1], "tm", 1)
        before = jnp.where(time_index == 0, initial, before)
        previous = jnp.concatenate([before[None], iterate[:-1]], axis=0)
        extended = with_halo(iterate, (("space", 1),), 1)
        extended = jnp.pad(extended, ((0, 0), (0, 0), (1, 1), (1, 1)))
        residual = (
            forcing
            - ((1.0 + 6.0 * coupling) * iterate - coupled(extended, coupling, advect))
            + previous
        )
        scaled = residual * time_weight
        spectrum = forward(lax.all_to_all(scaled, "tm", split_axis=2, concat_axis=0, tiled=True))
        blocked = lax.all_to_all(spectrum, "tm", split_axis=1, concat_axis=3, tiled=True)
        frequency = (time_index * local_steps + jnp.arange(local_steps, dtype=jnp.int32)).astype(
            jnp.float32
        )

        def extend_narrow(field):
            grown = with_halo(field, (("space", 2),), 1)
            return jnp.pad(grown, ((0, 0), (0, 0), (0, 0), (1, 1), (1, 1)))

        solved = jacobi(blocked, coupling, advect, frequency, total_steps, extend_narrow)
        spectrum_out = lax.all_to_all(solved, "tm", split_axis=3, concat_axis=1, tiled=True)
        inverse_part = (
            matmul(cosine, spectrum_out[0].reshape(total_steps, -1))
            - matmul(sine_table, spectrum_out[1].reshape(total_steps, -1))
        ) / total_steps
        inverse_part = inverse_part.reshape(spectrum_out.shape[1:])
        correction = lax.all_to_all(inverse_part, "tm", split_axis=0, concat_axis=2, tiled=True)
        iterate = iterate + correction / time_weight
    return iterate


def solution(mesh):
    return jax.shard_map(
        body,
        mesh=mesh,
        in_specs=(
            P("tm", "space", None, None),
            P("space", None, None),
            P("space", None, None),
            P(None, "space", None, None),
        ),
        out_specs=P("tm", "space", None, None),
        check_vma=False,
    )
```

profile of v0, /device:TPU:0, one launch (start us, length us, event | category | flops | bytes accessed | tf_op | source)
XLA Modules:
  0.0 317.9 jit_solution(9283185566868830685)
XLA Ops:
  0.0 2.5 collective-permute-start.2
  3.5 4.2 %collective-permute-start.1 = (f32[1,1,128,128]{3,2,1,0:T(8,128)S(1)}, f32[1,1,128,128]{3,2,1,0:T(8,128)S(1)}, u32[]{:S(2)}, u32[]{:S(2)}) collective-permute-start(f32[1,1,128,128]{3,2,1,0:T(8,128)S(1)} %get-tuple-element.86), channel_id=1, source_target_pairs={{0,1},{2,3},{4,5},{6,7},{8,9},{10,11},{12,13},{14,15},{16,17},{18,... | collective-permute-start | bytes 196616 | tf_op jit(solution)/shard_map/ppermute | solution.py:26
  10.4 3.7 %collective-permute-done = f32[1,1,128,128]{3,2,1,0:T(8,128)S(1)} collective-permute-done((f32[1,1,128,128]{3,2,1,0:T(8,128)S(1)}, f32[1,1,128,128]{3,2,1,0:T(8,128)S(1)}, u32[]{:S(2)}, u32[]{:S(2)}) %collective-permute-start) | collective-permute-done | bytes 65568 | tf_op jit(solution)/shard_map/ppermute | solution.py:29
  15.0 15.7 %all_to_all.108 = f32[1,4,128,128]{3,1,0,2:T(4,128)S(1)} all-to-all(f32[1,4,128,128]{3,1,0,2:T(4,128)S(1)} %copy.21), channel_id=1, replica_groups=mesh['tm'=16,'space'=2] {'tm'}, dimensions={2} | all-to-all | bytes 524288 | tf_op jit(solution)/shard_map/all_to_all | solution.py:115
  33.1 3.6 %all-to-all-start.1 = ((f32[2,16,4,8,128]{4,3,2,0,1:T(8,128)}), f32[2,16,4,8,128]{4,3,2,0,1:T(8,128)S(1)}, u32[]{:S(2)}, u32[]{:S(2)}) async-start(f32[2,16,4,8,128]{4,3,2,0,1:T(8,128)} %copy.25), calls=%async_computation.1 | async-start | bytes 1048576 | tf_op jit(solution)/shard_map/all_to_all | solution.py:116
  36.8 14.1 %all-to-all-done.1 = f32[2,16,4,8,128]{4,3,2,0,1:T(8,128)S(1)} async-done(((f32[2,16,4,8,128]{4,3,2,0,1:T(8,128)}), f32[2,16,4,8,128]{4,3,2,0,1:T(8,128)S(1)}, u32[]{:S(2)}, u32[]{:S(2)}) %all-to-all-start.1) | async-done | bytes 524320 | tf_op jit(solution)/shard_map/all_to_all | solution.py:116
  51.1 1.6 collective-permute-start.4
  54.0 1.7 collective-permute-done.4
  55.7 4.1 %collective-permute-done.3 = f32[2,1,1,128,128]{4,3,2,1,0:T(8,128)S(1)} collective-permute-done((f32[2,1,1,128,128]{4,3,2,1,0:T(8,128)S(1)}, f32[2,1,1,128,128]{4,3,2,1,0:T(8,128)S(1)}, u32[]{:S(2)}, u32[]{:S(2)}) %collective-permute-start.3) | collective-permute-done | bytes 131104 | tf_op jit(solution)/shard_map/ppermute | solution.py:29
  65.0 4.4 %collective-permute-done.5 = f32[2,1,1,128,128]{4,3,2,1,0:T(8,128)S(1)} collective-permute-done((f32[2,1,1,128,128]{4,3,2,1,0:T(8,128)S(1)}, f32[2,1,1,128,128]{4,3,2,1,0:T(8,128)S(1)}, u32[]{:S(2)}, u32[]{:S(2)}) %collective-permute-start.5) | collective-permute-done | bytes 131104 | tf_op jit(solution)/shard_map/ppermute | solution.py:29
  70.6 1.5 collective-permute-start.8
  74.6 4.4 %collective-permute-done.7 = f32[2,1,1,128,128]{4,3,2,1,0:T(8,128)S(1)} collective-permute-done((f32[2,1,1,128,128]{4,3,2,1,0:T(8,128)S(1)}, f32[2,1,1,128,128]{4,3,2,1,0:T(8,128)S(1)}, u32[]{:S(2)}, u32[]{:S(2)}) %collective-permute-start.7) | collective-permute-done | bytes 131104 | tf_op jit(solution)/shard_map/ppermute | solution.py:29
  80.3 1.5 collective-permute-start.10
  84.2 4.4 %collective-permute-done.9 = f32[2,1,1,128,128]{4,3,2,1,0:T(8,128)S(1)} collective-permute-done((f32[2,1,1,128,128]{4,3,2,1,0:T(8,128)S(1)}, f32[2,1,1,128,128]{4,3,2,1,0:T(8,128)S(1)}, u32[]{:S(2)}, u32[]{:S(2)}) %collective-permute-start.9) | collective-permute-done | bytes 131104 | tf_op jit(solution)/shard_map/ppermute | solution.py:29
  89.9 1.5 collective-permute-start.12
  93.9 4.4 %collective-permute-done.11 = f32[2,1,1,128,128]{4,3,2,1,0:T(8,128)S(1)} collective-permute-done((f32[2,1,1,128,128]{4,3,2,1,0:T(8,128)S(1)}, f32[2,1,1,128,128]{4,3,2,1,0:T(8,128)S(1)}, u32[]{:S(2)}, u32[]{:S(2)}) %collective-permute-start.11) | collective-permute-done | bytes 131104 | tf_op jit(solution)/shard_map/ppermute | solution.py:29
  99.5 1.5 collective-permute-start.14
  103.5 4.4 %collective-permute-done.13 = f32[2,1,1,128,128]{4,3,2,1,0:T(8,128)S(1)} collective-permute-done((f32[2,1,1,128,128]{4,3,2,1,0:T(8,128)S(1)}, f32[2,1,1,128,128]{4,3,2,1,0:T(8,128)S(1)}, u32[]{:S(2)}, u32[]{:S(2)}) %collective-permute-start.13) | collective-permute-done | bytes 131104 | tf_op jit(solution)/shard_map/ppermute | solution.py:29
  109.1 1.5 collective-permute-start.16
  110.6 1.5 collective-permute-start.15
  113.5 4.7 %collective-permute-done.15 = f32[2,1,1,128,128]{4,3,2,1,0:T(8,128)S(1)} collective-permute-done((f32[2,1,1,128,128]{4,3,2,1,0:T(8,128)S(1)}, f32[2,1,1,128,128]{4,3,2,1,0:T(8,128)S(1)}, u32[]{:S(2)}, u32[]{:S(2)}) %collective-permute-start.15) | collective-permute-done | bytes 131104 | tf_op jit(solution)/shard_map/ppermute | solution.py:29
  123.4 4.4 %collective-permute-done.17 = f32[2,1,1,128,128]{4,3,2,1,0:T(8,128)S(1)} collective-permute-done((f32[2,1,1,128,128]{4,3,2,1,0:T(8,128)S(1)}, f32[2,1,1,128,128]{4,3,2,1,0:T(8,128)S(1)}, u32[]{:S(2)}, u32[]{:S(2)}) %collective-permute-start.17) | collective-permute-done | bytes 131104 | tf_op jit(solution)/shard_map/ppermute | solution.py:29
  129.4 18.5 %all_to_all.109 = f32[2,1,4,128,128]{4,2,1,0,3:T(4,128)S(1)} all-to-all(f32[2,1,4,128,128]{4,2,1,0,3:T(4,128)S(1)} %copy.27), channel_id=1, replica_groups=mesh['tm'=16,'space'=2] {'tm'}, dimensions={3} | all-to-all | bytes 1048576 | tf_op jit(solution)/shard_map/all_to_all | solution.py:126
  149.1 14.0 %all_to_all.110 = f32[16,4,8,128]{3,2,1,0:T(8,128)S(1)} all-to-all(f32[16,4,8,128]{3,2,1,0:T(8,128)S(1)} %bitcast.743), channel_id=1, replica_groups=mesh['tm'=16,'space'=2] {'tm'}, dimensions={0} | all-to-all | bytes 524288 | tf_op jit(solution)/shard_map/all_to_all | solution.py:132
  163.1 1.8 collective-permute-start.21
  164.9 1.5 collective-permute-start.20
  168.3 4.3 %collective-permute-done.19 = f32[1,1,128,128]{3,2,1,0:T(8,128)S(1)} collective-permute-done((f32[1,1,128,128]{3,2,1,0:T(8,128)S(1)}, f32[1,1,128,128]{3,2,1,0:T(8,128)S(1)}, u32[]{:S(2)}, u32[]{:S(2)}) %collective-permute-start.19) | collective-permute-done | bytes 65568 | tf_op jit(solution)/shard_map/ppermute | solution.py:29
  173.4 13.0 %all_to_all.111 = f32[1,4,128,128]{3,1,0,2:T(4,128)S(1)} all-to-all(f32[1,4,128,128]{3,1,0,2:T(4,128)S(1)} %copy.30), channel_id=1, replica_groups=mesh['tm'=16,'space'=2] {'tm'}, dimensions={2} | all-to-all | bytes 524288 | tf_op jit(solution)/shard_map/all_to_all | solution.py:115
  188.0 17.0 %all_to_all.112 = f32[2,16,4,8,128]{4,3,2,0,1:T(8,128)S(1)} all-to-all(f32[2,16,4,8,128]{4,3,2,0,1:T(8,128)S(1)} %copy.34), channel_id=1, replica_groups=mesh['tm'=16,'space'=2] {'tm'}, dimensions={1} | all-to-all | bytes 1048576 | tf_op jit(solution)/shard_map/all_to_all | solution.py:116
  205.2 1.6 collective-permute-start.23
  208.1 1.7 collective-permute-done.23
  209.8 4.1 %collective-permute-done.22 = f32[2,1,1,128,128]{4,3,2,1,0:T(8,128)S(1)} collective-permute-done((f32[2,1,1,128,128]{4,3,2,1,0:T(8,128)S(1)}, f32[2,1,1,128,128]{4,3,2,1,0:T(8,128)S(1)}, u32[]{:S(2)}, u32[]{:S(2)}) %collective-permute-start.22) | collective-permute-done | bytes 131104 | tf_op jit(solution)/shard_map/ppermute | solution.py:29
  219.1 4.4 %collective-permute-done.24 = f32[2,1,1,128,128]{4,3,2,1,0:T(8,128)S(1)} collective-permute-done((f32[2,1,1,128,128]{4,3,2,1,0:T(8,128)S(1)}, f32[2,1,1,128,128]{4,3,2,1,0:T(8,128)S(1)}, u32[]{:S(2)}, u32[]{:S(2)}) %collective-permute-start.24) | collective-permute-done | bytes 131104 | tf_op jit(solution)/shard_map/ppermute | solution.py:29
  224.8 1.5 collective-permute-start.27
  228.7 4.4 %collective-permute-done.26 = f32[2,1,1,128,128]{4,3,2,1,0:T(8,128)S(1)} collective-permute-done((f32[2,1,1,128,128]{4,3,2,1,0:T(8,128)S(1)}, f32[2,1,1,128,128]{4,3,2,1,0:T(8,128)S(1)}, u32[]{:S(2)}, u32[]{:S(2)}) %collective-permute-start.26) | collective-permute-done | bytes 131104 | tf_op jit(solution)/shard_map/ppermute | solution.py:29
  234.4 1.5 collective-permute-start.29
  235.9 1.5 collective-permute-start.28
  238.4 4.4 %collective-permute-done.28 = f32[2,1,1,128,128]{4,3,2,1,0:T(8,128)S(1)} collective-permute-done((f32[2,1,1,128,128]{4,3,2,1,0:T(8,128)S(1)}, f32[2,1,1,128,128]{4,3,2,1,0:T(8,128)S(1)}, u32[]{:S(2)}, u32[]{:S(2)}) %collective-permute-start.28) | collective-permute-done | bytes 131104 | tf_op jit(solution)/shard_map/ppermute | solution.py:29
  244.0 1.5 collective-permute-start.31
  248.0 4.4 %collective-permute-done.30 = f32[2,1,1,128,128]{4,3,2,1,0:T(8,128)S(1)} collective-permute-done((f32[2,1,1,128,128]{4,3,2,1,0:T(8,128)S(1)}, f32[2,1,1,128,128]{4,3,2,1,0:T(8,128)S(1)}, u32[]{:S(2)}, u32[]{:S(2)}) %collective-permute-start.30) | collective-permute-done | bytes 131104 | tf_op jit(solution)/shard_map/ppermute | solution.py:29
  253.6 1.5 collective-permute-start.33
  257.6 4.4 %collective-permute-done.32 = f32[2,1,1,128,128]{4,3,2,1,0:T(8,128)S(1)} collective-permute-done((f32[2,1,1,128,128]{4,3,2,1,0:T(8,128)S(1)}, f32[2,1,1,128,128]{4,3,2,1,0:T(8,128)S(1)}, u32[]{:S(2)}, u32[]{:S(2)}) %collective-permute-start.32) | collective-permute-done | bytes 131104 | tf_op jit(solution)/shard_map/ppermute | solution.py:29
  263.2 1.5 collective-permute-start.35
  266.0 1.6 collective-permute-done.35
  267.6 4.7 %collective-permute-done.34 = f32[2,1,1,128,128]{4,3,2,1,0:T(8,128)S(1)} collective-permute-done((f32[2,1,1,128,128]{4,3,2,1,0:T(8,128)S(1)}, f32[2,1,1,128,128]{4,3,2,1,0:T(8,128)S(1)}, u32[]{:S(2)}, u32[]{:S(2)}) %collective-permute-start.34) | collective-permute-done | bytes 131104 | tf_op jit(solution)/shard_map/ppermute | solution.py:29
  277.5 4.4 %collective-permute-done.36 = f32[2,1,1,128,128]{4,3,2,1,0:T(8,128)S(1)} collective-permute-done((f32[2,1,1,128,128]{4,3,2,1,0:T(8,128)S(1)}, f32[2,1,1,128,128]{4,3,2,1,0:T(8,128)S(1)}, u32[]{:S(2)}, u32[]{:S(2)}) %collective-permute-start.36) | collective-permute-done | bytes 131104 | tf_op jit(solution)/shard_map/ppermute | solution.py:29
  283.5 18.5 %all_to_all.113 = f32[2,1,4,128,128]{4,2,1,0,3:T(4,128)S(1)} all-to-all(f32[2,1,4,128,128]{4,2,1,0,3:T(4,128)S(1)} %copy.36), channel_id=1, replica_groups=mesh['tm'=16,'space'=2] {'tm'}, dimensions={3} | all-to-all | bytes 1048576 | tf_op jit(solution)/shard_map/all_to_all | solution.py:126
  303.2 14.0 %all_to_all.114 = f32[16,4,8,128]{3,2,1,0:T(8,128)S(1)} all-to-all(f32[16,4,8,128]{3,2,1,0:T(8,128)S(1)} %bitcast.748), channel_id=1, replica_groups=mesh['tm'=16,'space'=2] {'tm'}, dimensions={0} | all-to-all | bytes 524288 | tf_op jit(solution)/shard_map/all_to_all | solution.py:132
  (158 shorter events, 74.2 us)
Async XLA Ops:
  0.0 14.1 %copy-start.1 = (f32[4,128,128]{2,1,0:T(8,128)S(1)}, f32[4,128,128]{2,1,0:T(8,128)}, u32[]{:S(2)}) copy-start(f32[4,128,128]{2,1,0:T(8,128)} %param.5) | copy-start | bytes 786436
  0.0 14.4 %collective-permute-start.2 = (f32[4,128,128]{2,1,0:T(8,128)}, f32[4,128,128]{2,1,0:T(8,128)S(1)}, u32[]{:S(2)}, u32[]{:S(2)}) collective-permute-start(f32[4,128,128]{2,1,0:T(8,128)} %param.5), channel_id=1, source_target_pairs={{0,2},{2,4},{4,6},{6,8},{8,10},{10,12},{12,14},{14,16},{16,18},{18... | collective-permute-start | bytes 786440 | tf_op jit(solution)/shard_map/ppermute | solution.py:18
  2.5 11.9 %copy-start = (f32[4,128,128]{2,1,0:T(8,128)S(1)}, f32[4,128,128]{2,1,0:T(8,128)}, u32[]{:S(2)}) copy-start(f32[4,128,128]{2,1,0:T(8,128)} %param.6) | copy-start | bytes 786436
  2.6 11.9 %copy-start.2 = (f32[1,4,128,128]{3,2,1,0:T(8,128)S(1)}, f32[1,4,128,128]{3,2,1,0:T(8,128)}, u32[]{:S(2)}) copy-start(f32[1,4,128,128]{3,2,1,0:T(8,128)} %param.4) | copy-start | bytes 786436
  3.5 6.9 %collective-permute-start.1 = (f32[1,1,128,128]{3,2,1,0:T(8,128)S(1)}, f32[1,1,128,128]{3,2,1,0:T(8,128)S(1)}, u32[]{:S(2)}, u32[]{:S(2)}) collective-permute-start(f32[1,1,128,128]{3,2,1,0:T(8,128)S(1)} %get-tuple-element.86), channel_id=1, source_target_pairs={{0,1},{2,3},{4,5},{6,7},{8,9},{10,11},{12,13},{14,15},{16,17},{18,... | collective-permute-start | bytes 196616 | tf_op jit(solution)/shard_map/ppermute | solution.py:26
  7.8 6.4 %collective-permute-start = (f32[1,1,128,128]{3,2,1,0:T(8,128)S(1)}, f32[1,1,128,128]{3,2,1,0:T(8,128)S(1)}, u32[]{:S(2)}, u32[]{:S(2)}) collective-permute-start(f32[1,1,128,128]{3,2,1,0:T(8,128)S(1)} %get-tuple-element.87), channel_id=1, source_target_pairs={{1,0},{3,2},{5,4},{7,6},{9,8},{11,10},{13,12},{15,14},{17,16},{19,... | collective-permute-start | bytes 196616 | tf_op jit(solution)/shard_map/ppermute | solution.py:29
  33.1 17.8 %all-to-all-start.1 = ((f32[2,16,4,8,128]{4,3,2,0,1:T(8,128)}), f32[2,16,4,8,128]{4,3,2,0,1:T(8,128)S(1)}, u32[]{:S(2)}, u32[]{:S(2)}) async-start(f32[2,16,4,8,128]{4,3,2,0,1:T(8,128)} %copy.25), calls=%async_computation.1 | async-start | bytes 1048576 | tf_op jit(solution)/shard_map/all_to_all | solution.py:116
  51.1 4.6 %collective-permute-start.4 = (f32[2,1,1,128,128]{4,3,2,1,0:T(8,128)S(1)}, f32[2,1,1,128,128]{4,3,2,1,0:T(8,128)S(1)}, u32[]{:S(2)}, u32[]{:S(2)}) collective-permute-start(f32[2,1,1,128,128]{4,3,2,1,0:T(8,128)S(1)} %get-tuple-element.82), channel_id=1, source_target_pairs={{0,1},{2,3},{4,5},{6,7},{8,9},{10,11},{12,13},{14,15},{16,17},{18,... | collective-permute-start | bytes 393224 | tf_op jit(solution)/shard_map/ppermute | solution.py:26
  52.7 7.1 %collective-permute-start.3 = (f32[2,1,1,128,128]{4,3,2,1,0:T(8,128)S(1)}, f32[2,1,1,128,128]{4,3,2,1,0:T(8,128)S(1)}, u32[]{:S(2)}, u32[]{:S(2)}) collective-permute-start(f32[2,1,1,128,128]{4,3,2,1,0:T(8,128)S(1)} %get-tuple-element.83), channel_id=1, source_target_pairs={{1,0},{3,2},{5,4},{7,6},{9,8},{11,10},{13,12},{15,14},{17,16},{19,... | collective-permute-start | bytes 393224 | tf_op jit(solution)/shard_map/ppermute | solution.py:29
  61.1 4.0 %collective-permute-start.6 = (f32[2,1,1,128,128]{4,3,2,1,0:T(8,128)S(1)}, f32[2,1,1,128,128]{4,3,2,1,0:T(8,128)S(1)}, u32[]{:S(2)}, u32[]{:S(2)}) collective-permute-start(f32[2,1,1,128,128]{4,3,2,1,0:T(8,128)S(1)} %get-tuple-element.80), channel_id=1, source_target_pairs={{0,1},{2,3},{4,5},{6,7},{8,9},{10,11},{12,13},{14,15},{16,17},{18,... | collective-permute-start | bytes 393224 | tf_op jit(solution)/shard_map/ppermute | solution.py:26
  62.5 6.9 %collective-permute-start.5 = (f32[2,1,1,128,128]{4,3,2,1,0:T(8,128)S(1)}, f32[2,1,1,128,128]{4,3,2,1,0:T(8,128)S(1)}, u32[]{:S(2)}, u32[]{:S(2)}) collective-permute-start(f32[2,1,1,128,128]{4,3,2,1,0:T(8,128)S(1)} %get-tuple-element.81), channel_id=1, source_target_pairs={{1,0},{3,2},{5,4},{7,6},{9,8},{11,10},{13,12},{15,14},{17,16},{19,... | collective-permute-start | bytes 393224 | tf_op jit(solution)/shard_map/ppermute | solution.py:29
  70.6 4.0 %collective-permute-start.8 = (f32[2,1,1,128,128]{4,3,2,1,0:T(8,128)S(1)}, f32[2,1,1,128,128]{4,3,2,1,0:T(8,128)S(1)}, u32[]{:S(2)}, u32[]{:S(2)}) collective-permute-start(f32[2,1,1,128,128]{4,3,2,1,0:T(8,128)S(1)} %get-tuple-element.78), channel_id=1, source_target_pairs={{0,1},{2,3},{4,5},{6,7},{8,9},{10,11},{12,13},{14,15},{16,17},{18,... | collective-permute-start | bytes 393224 | tf_op jit(solution)/shard_map/ppermute | solution.py:26
  72.1 6.9 %collective-permute-start.7 = (f32[2,1,1,128,128]{4,3,2,1,0:T(8,128)S(1)}, f32[2,1,1,128,128]{4,3,2,1,0:T(8,128)S(1)}, u32[]{:S(2)}, u32[]{:S(2)}) collective-permute-start(f32[2,1,1,128,128]{4,3,2,1,0:T(8,128)S(1)} %get-tuple-element.79), channel_id=1, source_target_pairs={{1,0},{3,2},{5,4},{7,6},{9,8},{11,10},{13,12},{15,14},{17,16},{19,... | collective-permute-start | bytes 393224 | tf_op jit(solution)/shard_map/ppermute | solution.py:29
  80.3 4.0 %collective-permute-start.10 = (f32[2,1,1,128,128]{4,3,2,1,0:T(8,128)S(1)}, f32[2,1,1,128,128]{4,3,2,1,0:T(8,128)S(1)}, u32[]{:S(2)}, u32[]{:S(2)}) collective-permute-start(f32[2,1,1,128,128]{4,3,2,1,0:T(8,128)S(1)} %get-tuple-element.76), channel_id=1, source_target_pairs={{0,1},{2,3},{4,5},{6,7},{8,9},{10,11},{12,13},{14,15},{16,17},{18,... | collective-permute-start | bytes 393224 | tf_op jit(solution)/shard_map/ppermute | solution.py:26
  81.8 6.9 %collective-permute-start.9 = (f32[2,1,1,128,128]{4,3,2,1,0:T(8,128)S(1)}, f32[2,1,1,128,128]{4,3,2,1,0:T(8,128)S(1)}, u32[]{:S(2)}, u32[]{:S(2)}) collective-permute-start(f32[2,1,1,128,128]{4,3,2,1,0:T(8,128)S(1)} %get-tuple-element.77), channel_id=1, source_target_pairs={{1,0},{3,2},{5,4},{7,6},{9,8},{11,10},{13,12},{15,14},{17,16},{19,... | collective-permute-start | bytes 393224 | tf_op jit(solution)/shard_map/ppermute | solution.py:29
  89.9 4.0 %collective-permute-start.12 = (f32[2,1,1,128,128]{4,3,2,1,0:T(8,128)S(1)}, f32[2,1,1,128,128]{4,3,2,1,0:T(8,128)S(1)}, u32[]{:S(2)}, u32[]{:S(2)}) collective-permute-start(f32[2,1,1,128,128]{4,3,2,1,0:T(8,128)S(1)} %get-tuple-element.74), channel_id=1, source_target_pairs={{0,1},{2,3},{4,5},{6,7},{8,9},{10,11},{12,13},{14,15},{16,17},{18,... | collective-permute-start | bytes 393224 | tf_op jit(solution)/shard_map/ppermute | solution.py:26
  91.4 6.9 %collective-permute-start.11 = (f32[2,1,1,128,128]{4,3,2,1,0:T(8,128)S(1)}, f32[2,1,1,128,128]{4,3,2,1,0:T(8,128)S(1)}, u32[]{:S(2)}, u32[]{:S(2)}) collective-permute-start(f32[2,1,1,128,128]{4,3,2,1,0:T(8,128)S(1)} %get-tuple-element.75), channel_id=1, source_target_pairs={{1,0},{3,2},{5,4},{7,6},{9,8},{11,10},{13,12},{15,14},{17,16},{19,... | collective-permute-start | bytes 393224 | tf_op jit(solution)/shard_map/ppermute | solution.py:29
  99.5 4.0 %collective-permute-start.14 = (f32[2,1,1,128,128]{4,3,2,1,0:T(8,128)S(1)}, f32[2,1,1,128,128]{4,3,2,1,0:T(8,128)S(1)}, u32[]{:S(2)}, u32[]{:S(2)}) collective-permute-start(f32[2,1,1,128,128]{4,3,2,1,0:T(8,128)S(1)} %get-tuple-element.72), channel_id=1, source_target_pairs={{0,1},{2,3},{4,5},{6,7},{8,9},{10,11},{12,13},{14,15},{16,17},{18,... | collective-permute-start | bytes 393224 | tf_op jit(solution)/shard_map/ppermute | solution.py:26
  101.0 6.9 %collective-permute-start.13 = (f32[2,1,1,128,128]{4,3,2,1,0:T(8,128)S(1)}, f32[2,1,1,128,128]{4,3,2,1,0:T(8,128)S(1)}, u32[]{:S(2)}, u32[]{:S(2)}) collective-permute-start(f32[2,1,1,128,128]{4,3,2,1,0:T(8,128)S(1)} %get-tuple-element.73), channel_id=1, source_target_pairs={{1,0},{3,2},{5,4},{7,6},{9,8},{11,10},{13,12},{15,14},{17,16},{19,... | collective-permute-start | bytes 393224 | tf_op jit(solution)/shard_map/ppermute | solution.py:29
  109.1 4.4 %collective-permute-start.16 = (f32[2,1,1,128,128]{4,3,2,1,0:T(8,128)S(1)}, f32[2,1,1,128,128]{4,3,2,1,0:T(8,128)S(1)}, u32[]{:S(2)}, u32[]{:S(2)}) collective-permute-start(f32[2,1,1,128,128]{4,3,2,1,0:T(8,128)S(1)} %get-tuple-element.70), channel_id=1, source_target_pairs={{0,1},{2,3},{4,5},{6,7},{8,9},{10,11},{12,13},{14,15},{16,17},{18,... | collective-permute-start | bytes 393224 | tf_op jit(solution)/shard_map/ppermute | solution.py:26
  110.6 7.6 %collective-permute-start.15 = (f32[2,1,1,128,128]{4,3,2,1,0:T(8,128)S(1)}, f32[2,1,1,128,128]{4,3,2,1,0:T(8,128)S(1)}, u32[]{:S(2)}, u32[]{:S(2)}) collective-permute-start(f32[2,1,1,128,128]{4,3,2,1,0:T(8,128)S(1)} %get-tuple-element.71), channel_id=1, source_target_pairs={{1,0},{3,2},{5,4},{7,6},{9,8},{11,10},{13,12},{15,14},{17,16},{19,... | collective-permute-start | bytes 393224 | tf_op jit(solution)/shard_map/ppermute | solution.py:29
  119.4 4.0 %collective-permute-start.18 = (f32[2,1,1,128,128]{4,3,2,1,0:T(8,128)S(1)}, f32[2,1,1,128,128]{4,3,2,1,0:T(8,128)S(1)}, u32[]{:S(2)}, u32[]{:S(2)}) collective-permute-start(f32[2,1,1,128,128]{4,3,2,1,0:T(8,128)S(1)} %get-tuple-element.68), channel_id=1, source_target_pairs={{0,1},{2,3},{4,5},{6,7},{8,9},{10,11},{12,13},{14,15},{16,17},{18,... | collective-permute-start | bytes 393224 | tf_op jit(solution)/shard_map/ppermute | solution.py:26
  120.9 6.9 %collective-permute-start.17 = (f32[2,1,1,128,128]{4,3,2,1,0:T(8,128)S(1)}, f32[2,1,1,128,128]{4,3,2,1,0:T(8,128)S(1)}, u32[]{:S(2)}, u32[]{:S(2)}) collective-permute-start(f32[2,1,1,128,128]{4,3,2,1,0:T(8,128)S(1)} %get-tuple-element.69), channel_id=1, source_target_pairs={{1,0},{3,2},{5,4},{7,6},{9,8},{11,10},{13,12},{15,14},{17,16},{19,... | collective-permute-start | bytes 393224 | tf_op jit(solution)/shard_map/ppermute | solution.py:29
  163.1 9.8 %collective-permute-start.21 = (f32[4,128,128]{2,1,0:T(8,128)S(1)}, f32[4,128,128]{2,1,0:T(8,128)S(1)}, u32[]{:S(2)}, u32[]{:S(2)}) collective-permute-start(f32[4,128,128]{2,1,0:T(8,128)S(1)} %bitcast_add_fusion.1), channel_id=1, source_target_pairs={{0,2},{2,4},{4,6},{6,8},{8,10},{10,12},{12,14},{14,16},{16,18},{18... | collective-permute-start | bytes 786440 | tf_op jit(solution)/shard_map/ppermute | solution.py:18
  164.9 3.4 %collective-permute-start.20 = (f32[1,1,128,128]{3,2,1,0:T(8,128)S(1)}, f32[1,1,128,128]{3,2,1,0:T(8,128)S(1)}, u32[]{:S(2)}, u32[]{:S(2)}) collective-permute-start(f32[1,1,128,128]{3,2,1,0:T(8,128)S(1)} %get-tuple-element.84), channel_id=1, source_target_pairs={{0,1},{2,3},{4,5},{6,7},{8,9},{10,11},{12,13},{14,15},{16,17},{18,... | collective-permute-start | bytes 196616 | tf_op jit(solution)/shard_map/ppermute | solution.py:26
  166.4 6.2 %collective-permute-start.19 = (f32[1,1,128,128]{3,2,1,0:T(8,128)S(1)}, f32[1,1,128,128]{3,2,1,0:T(8,128)S(1)}, u32[]{:S(2)}, u32[]{:S(2)}) collective-permute-start(f32[1,1,128,128]{3,2,1,0:T(8,128)S(1)} %get-tuple-element.85), channel_id=1, source_target_pairs={{1,0},{3,2},{5,4},{7,6},{9,8},{11,10},{13,12},{15,14},{17,16},{19,... | collective-permute-start | bytes 196616 | tf_op jit(solution)/shard_map/ppermute | solution.py:29
  205.2 4.6 %collective-permute-start.23 = (f32[2,1,1,128,128]{4,3,2,1,0:T(8,128)S(1)}, f32[2,1,1,128,128]{4,3,2,1,0:T(8,128)S(1)}, u32[]{:S(2)}, u32[]{:S(2)}) collective-permute-start(f32[2,1,1,128,128]{4,3,2,1,0:T(8,128)S(1)} %get-tuple-element.64), channel_id=1, source_target_pairs={{0,1},{2,3},{4,5},{6,7},{8,9},{10,11},{12,13},{14,15},{16,17},{18,... | collective-permute-start | bytes 393224 | tf_op jit(solution)/shard_map/ppermute | solution.py:26
  206.8 7.2 %collective-permute-start.22 = (f32[2,1,1,128,128]{4,3,2,1,0:T(8,128)S(1)}, f32[2,1,1,128,128]{4,3,2,1,0:T(8,128)S(1)}, u32[]{:S(2)}, u32[]{:S(2)}) collective-permute-start(f32[2,1,1,128,128]{4,3,2,1,0:T(8,128)S(1)} %get-tuple-element.65), channel_id=1, source_target_pairs={{1,0},{3,2},{5,4},{7,6},{9,8},{11,10},{13,12},{15,14},{17,16},{19,... | collective-permute-start | bytes 393224 | tf_op jit(solution)/shard_map/ppermute | solution.py:29
  215.2 4.0 %collective-permute-start.25 = (f32[2,1,1,128,128]{4,3,2,1,0:T(8,128)S(1)}, f32[2,1,1,128,128]{4,3,2,1,0:T(8,128)S(1)}, u32[]{:S(2)}, u32[]{:S(2)}) collective-permute-start(f32[2,1,1,128,128]{4,3,2,1,0:T(8,128)S(1)} %get-tuple-element.62), channel_id=1, source_target_pairs={{0,1},{2,3},{4,5},{6,7},{8,9},{10,11},{12,13},{14,15},{16,17},{18,... | collective-permute-start | bytes 393224 | tf_op jit(solution)/shard_map/ppermute | solution.py:26
  216.6 6.9 %collective-permute-start.24 = (f32[2,1,1,128,128]{4,3,2,1,0:T(8,128)S(1)}, f32[2,1,1,128,128]{4,3,2,1,0:T(8,128)S(1)}, u32[]{:S(2)}, u32[]{:S(2)}) collective-permute-start(f32[2,1,1,128,128]{4,3,2,1,0:T(8,128)S(1)} %get-tuple-element.63), channel_id=1, source_target_pairs={{1,0},{3,2},{5,4},{7,6},{9,8},{11,10},{13,12},{15,14},{17,16},{19,... | collective-permute-start | bytes 393224 | tf_op jit(solution)/shard_map/ppermute | solution.py:29
  224.8 4.0 %collective-permute-start.27 = (f32[2,1,1,128,128]{4,3,2,1,0:T(8,128)S(1)}, f32[2,1,1,128,128]{4,3,2,1,0:T(8,128)S(1)}, u32[]{:S(2)}, u32[]{:S(2)}) collective-permute-start(f32[2,1,1,128,128]{4,3,2,1,0:T(8,128)S(1)} %get-tuple-element.60), channel_id=1, source_target_pairs={{0,1},{2,3},{4,5},{6,7},{8,9},{10,11},{12,13},{14,15},{16,17},{18,... | collective-permute-start | bytes 393224 | tf_op jit(solution)/shard_map/ppermute | solution.py:26
  226.3 6.9 %collective-permute-start.26 = (f32[2,1,1,128,128]{4,3,2,1,0:T(8,128)S(1)}, f32[2,1,1,128,128]{4,3,2,1,0:T(8,128)S(1)}, u32[]{:S(2)}, u32[]{:S(2)}) collective-permute-start(f32[2,1,1,128,128]{4,3,2,1,0:T(8,128)S(1)} %get-tuple-element.61), channel_id=1, source_target_pairs={{1,0},{3,2},{5,4},{7,6},{9,8},{11,10},{13,12},{15,14},{17,16},{19,... | collective-permute-start | bytes 393224 | tf_op jit(solution)/shard_map/ppermute | solution.py:29
  234.4 4.0 %collective-permute-start.29 = (f32[2,1,1,128,128]{4,3,2,1,0:T(8,128)S(1)}, f32[2,1,1,128,128]{4,3,2,1,0:T(8,128)S(1)}, u32[]{:S(2)}, u32[]{:S(2)}) collective-permute-start(f32[2,1,1,128,128]{4,3,2,1,0:T(8,128)S(1)} %get-tuple-element.58), channel_id=1, source_target_pairs={{0,1},{2,3},{4,5},{6,7},{8,9},{10,11},{12,13},{14,15},{16,17},{18,... | collective-permute-start | bytes 393224 | tf_op jit(solution)/shard_map/ppermute | solution.py:26
  235.9 6.9 %collective-permute-start.28 = (f32[2,1,1,128,128]{4,3,2,1,0:T(8,128)S(1)}, f32[2,1,1,128,128]{4,3,2,1,0:T(8,128)S(1)}, u32[]{:S(2)}, u32[]{:S(2)}) collective-permute-start(f32[2,1,1,128,128]{4,3,2,1,0:T(8,128)S(1)} %get-tuple-element.59), channel_id=1, source_target_pairs={{1,0},{3,2},{5,4},{7,6},{9,8},{11,10},{13,12},{15,14},{17,16},{19,... | collective-permute-start | bytes 393224 | tf_op jit(solution)/shard_map/ppermute | solution.py:29
  244.0 4.0 %collective-permute-start.31 = (f32[2,1,1,128,128]{4,3,2,1,0:T(8,128)S(1)}, f32[2,1,1,128,128]{4,3,2,1,0:T(8,128)S(1)}, u32[]{:S(2)}, u32[]{:S(2)}) collective-permute-start(f32[2,1,1,128,128]{4,3,2,1,0:T(8,128)S(1)} %get-tuple-element.56), channel_id=1, source_target_pairs={{0,1},{2,3},{4,5},{6,7},{8,9},{10,11},{12,13},{14,15},{16,17},{18,... | collective-permute-start | bytes 393224 | tf_op jit(solution)/shard_map/ppermute | solution.py:26
  245.5 6.9 %collective-permute-start.30 = (f32[2,1,1,128,128]{4,3,2,1,0:T(8,128)S(1)}, f32[2,1,1,128,128]{4,3,2,1,0:T(8,128)S(1)}, u32[]{:S(2)}, u32[]{:S(2)}) collective-permute-start(f32[2,1,1,128,128]{4,3,2,1,0:T(8,128)S(1)} %get-tuple-element.57), channel_id=1, source_target_pairs={{1,0},{3,2},{5,4},{7,6},{9,8},{11,10},{13,12},{15,14},{17,16},{19,... | collective-permute-start | bytes 393224 | tf_op jit(solution)/shard_map/ppermute | solution.py:29
  253.6 4.0 %collective-permute-start.33 = (f32[2,1,1,128,128]{4,3,2,1,0:T(8,128)S(1)}, f32[2,1,1,128,128]{4,3,2,1,0:T(8,128)S(1)}, u32[]{:S(2)}, u32[]{:S(2)}) collective-permute-start(f32[2,1,1,128,128]{4,3,2,1,0:T(8,128)S(1)} %get-tuple-element.54), channel_id=1, source_target_pairs={{0,1},{2,3},{4,5},{6,7},{8,9},{10,11},{12,13},{14,15},{16,17},{18,... | collective-permute-start | bytes 393224 | tf_op jit(solution)/shard_map/ppermute | solution.py:26
  255.1 6.9 %collective-permute-start.32 = (f32[2,1,1,128,128]{4,3,2,1,0:T(8,128)S(1)}, f32[2,1,1,128,128]{4,3,2,1,0:T(8,128)S(1)}, u32[]{:S(2)}, u32[]{:S(2)}) collective-permute-start(f32[2,1,1,128,128]{4,3,2,1,0:T(8,128)S(1)} %get-tuple-element.55), channel_id=1, source_target_pairs={{1,0},{3,2},{5,4},{7,6},{9,8},{11,10},{13,12},{15,14},{17,16},{19,... | collective-permute-start | bytes 393224 | tf_op jit(solution)/shard_map/ppermute | solution.py:29
  263.2 4.4 %collective-permute-start.35 = (f32[2,1,1,128,128]{4,3,2,1,0:T(8,128)S(1)}, f32[2,1,1,128,128]{4,3,2,1,0:T(8,128)S(1)}, u32[]{:S(2)}, u32[]{:S(2)}) collective-permute-start(f32[2,1,1,128,128]{4,3,2,1,0:T(8,128)S(1)} %get-tuple-element.52), channel_id=1, source_target_pairs={{0,1},{2,3},{4,5},{6,7},{8,9},{10,11},{12,13},{14,15},{16,17},{18,... | collective-permute-start | bytes 393224 | tf_op jit(solution)/shard_map/ppermute | solution.py:26
  264.7 7.6 %collective-permute-start.34 = (f32[2,1,1,128,128]{4,3,2,1,0:T(8,128)S(1)}, f32[2,1,1,128,128]{4,3,2,1,0:T(8,128)S(1)}, u32[]{:S(2)}, u32[]{:S(2)}) collective-permute-start(f32[2,1,1,128,128]{4,3,2,1,0:T(8,128)S(1)} %get-tuple-element.53), channel_id=1, source_target_pairs={{1,0},{3,2},{5,4},{7,6},{9,8},{11,10},{13,12},{15,14},{17,16},{19,... | collective-permute-start | bytes 393224 | tf_op jit(solution)/shard_map/ppermute | solution.py:29
  273.5 4.0 %collective-permute-start.37 = (f32[2,1,1,128,128]{4,3,2,1,0:T(8,128)S(1)}, f32[2,1,1,128,128]{4,3,2,1,0:T(8,128)S(1)}, u32[]{:S(2)}, u32[]{:S(2)}) collective-permute-start(f32[2,1,1,128,128]{4,3,2,1,0:T(8,128)S(1)} %get-tuple-element.50), channel_id=1, source_target_pairs={{0,1},{2,3},{4,5},{6,7},{8,9},{10,11},{12,13},{14,15},{16,17},{18,... | collective-permute-start | bytes 393224 | tf_op jit(solution)/shard_map/ppermute | solution.py:26
  275.0 6.9 %collective-permute-start.36 = (f32[2,1,1,128,128]{4,3,2,1,0:T(8,128)S(1)}, f32[2,1,1,128,128]{4,3,2,1,0:T(8,128)S(1)}, u32[]{:S(2)}, u32[]{:S(2)}) collective-permute-start(f32[2,1,1,128,128]{4,3,2,1,0:T(8,128)S(1)} %get-tuple-element.51), channel_id=1, source_target_pairs={{1,0},{3,2},{5,4},{7,6},{9,8},{11,10},{13,12},{15,14},{17,16},{19,... | collective-permute-start | bytes 393224 | tf_op jit(solution)/shard_map/ppermute | solution.py:29
where the time goes:
time: 319 us; the launch traced here: 318 us
  waiting for transfers between devices  113 us (35%)
  blocking collectives  111 us (35%)
  starting transfers between devices  61.2 us (19%)
  other arithmetic  23.6 us (7%)
  local copies, waits for them, and re-layouts  4.47 us (1%)
  matrix products  3.5 us (1%)
    ppermute x18, waiting for transfers between devices, with_halo(): lax.ppermute(lax.slice_in_dim(block, 0, width, axis=dim), axis, backward)  78 us
    all_to_all x2, blocking collectives, body(): lax.all_to_all(solved, 'tm', split_axis=3, concat_axis=1, tiled=True)  37 us
    ppermute x18, starting transfers between devices, with_halo(): lax.ppermute(lax.slice_in_dim(block, block.shape[dim] - width, None, axis...  29.6 us
    all_to_all x2, blocking collectives, body(): lax.all_to_all(scaled, 'tm', split_axis=2, concat_axis=0, tiled=True)  28.7 us
    all_to_all x2, blocking collectives, body(): lax.all_to_all(inverse_part, 'tm', split_axis=0, concat_axis=2, tiled=True)  28 us
    ppermute x18, starting transfers between devices, with_halo(): lax.ppermute(lax.slice_in_dim(block, 0, width, axis=dim), axis, backward)  23.7 us
    ppermute x18, waiting for transfers between devices, with_halo(): lax.ppermute(lax.slice_in_dim(block, block.shape[dim] - width, None, axis...  21.2 us
    all_to_all x1, blocking collectives, body(): lax.all_to_all(spectrum, 'tm', split_axis=1, concat_axis=3, tiled=True)  17 us
  transfers between devices with their start and end apart: 39, of which 36 were waited for; matrix products, arithmetic and copies ran while one was open for 1% of the time, Pallas kernels for 0%

commit v1 on v0

v1 whole, which is shorter than its diff:
```python
import math

import jax
import jax.numpy as jnp
import numpy as np
from jax import lax
from jax.experimental import pallas as pl
from jax.experimental.pallas import tpu as pltpu
from jax.sharding import PartitionSpec as P

ITERS = 2
SWEEPS = 8
HALO = 8

wrap_alpha = 0.1


def forward_table(steps):
    n = np.arange(steps)
    gamma = wrap_alpha ** (n / steps)
    table = np.zeros((steps // 2, 2, steps))
    for u in range(steps // 2):
        angle = 2.0 * np.pi * ((u * n) % steps) / steps
        if u == 0:
            table[u, 0] = gamma
            table[u, 1] = (1.0 - 2.0 * (n % 2)) * gamma
        else:
            table[u, 0] = np.cos(angle) * gamma
            table[u, 1] = -np.sin(angle) * gamma
    return table


def inverse_table(steps):
    n = np.arange(steps)
    table = np.zeros((steps // 2, 2, steps))
    for u in range(steps // 2):
        angle = 2.0 * np.pi * ((u * n) % steps) / steps
        if u == 0:
            table[u, 0] = 1.0 / steps
            table[u, 1] = (1.0 - 2.0 * (n % 2)) / steps
        else:
            table[u, 0] = 2.0 * np.cos(angle) / steps
            table[u, 1] = -2.0 * np.sin(angle) / steps
    return table


def by_index(index, values):
    picked = jnp.float32(values[0])
    for at in range(1, len(values)):
        picked = jnp.where(index == at, jnp.float32(values[at]), picked)
    return picked


def kernel(
    dims,
    f_ref,
    k_ref,
    out_ref,
    times,
    fields,
    edge,
    kbuf,
    coef,
    pq,
    src,
    wa,
    wb,
    whalo,
    part,
    gathered,
    reduced,
    last,
    back,
    states,
    s1,
    r1,
    s2,
    r2,
    sk,
    rk,
    se,
    re,
    sw,
    rw,
    ss,
    rs,
    sg,
    rg,
    s3,
    r3,
    s4,
    r4,
):
    T, S, NY, NX, zl = dims
    U = T // 2
    NZ = zl * S
    C = zl * NY // T
    bands = 2 * S
    R = NY // bands
    RH = R + 2 * HALO
    q = C // R
    per_plane = NY // C
    planes = NZ // U
    rho = wrap_alpha ** (1.0 / T)
    forward = forward_table(T)
    inverse = inverse_table(T)
    n = np.arange(T)
    gamma = wrap_alpha ** (n / T)

    t = lax.axis_index("tm")
    s = lax.axis_index("space")
    unit = t // 2
    core = t % 2
    band = s * 2 + core
    zi = t // per_plane
    row0 = pl.multiple_of((t % per_plane) * C, 8)

    def device(tt, ts):
        return {"tm": tt, "space": ts}

    def remote(source, target, ssem, rsem, tt, ts):
        return pltpu.make_async_remote_copy(
            src_ref=source,
            dst_ref=target,
            send_sem=ssem,
            recv_sem=rsem,
            device_id=device(tt, ts),
            device_id_type=pl.DeviceIdType.MESH,
        )

    sent = []

    def send(source, target, ssem, rsem, tt, ts, valid=None, maybe_self=True):
        copy = remote(source, target, ssem, rsem, tt, ts)
        same = jnp.logical_and(tt == t, ts == s) if maybe_self else None
        away = valid
        if maybe_self:
            here = same if valid is None else jnp.logical_and(valid, same)
            away = jnp.logical_not(same)
            if valid is not None:
                away = jnp.logical_and(valid, away)

            @pl.when(here)
            def _():
                pltpu.make_async_copy(source, target, rsem).start()

        if away is None:
            copy.start()
            sent.append(copy.wait_send)
        else:

            @pl.when(away)
            def _():
                copy.start()

            def finish():
                @pl.when(away)
                def _():
                    copy.wait_send()

            sent.append(finish)

    def arrived(target, rsem, valid=None):
        if valid is None:
            pltpu.make_async_copy(target, target, rsem).wait()
        else:

            @pl.when(valid)
            def _():
                pltpu.make_async_copy(target, target, rsem).wait()

    for d in range(1, T):
        tt = lax.rem(t + d, T)
        send(
            f_ref.at[pl.ds(pl.multiple_of(tt * C, 8), C)],
            times.at[t],
            s1.at[d],
            r1.at[d],
            tt,
            s,
            maybe_self=False,
        )
    send(
        k_ref.at[4, zl - 1, pl.ds(row0 + HALO, C)],
        edge.at[0],
        se.at[0],
        re.at[0],
        t,
        jnp.minimum(s + 1, S - 1),
        valid=s + 1 < S,
        maybe_self=False,
    )
    send(
        k_ref.at[4, 0, pl.ds(row0 + HALO, C)],
        edge.at[1],
        se.at[1],
        re.at[1],
        t,
        jnp.maximum(s - 1, 0),
        valid=s > 0,
        maybe_self=False,
    )
    for d in range(S):
        ts = lax.rem(s + d, S)
        rows = pl.ds(pl.multiple_of((ts * 2 + core) * R, 8), RH)
        source = k_ref.at[pl.ds(0, 4), :, rows]
        target = kbuf.at[:, pl.ds(s * zl, zl)]
        if d:
            send(source, target, sk.at[d], rk.at[d], t, ts, maybe_self=False)
        else:
            pltpu.make_async_copy(source, target, rk.at[0]).start()
    times[pl.ds(t, 1)] = f_ref[pl.ds(pl.multiple_of(t * C, 8), C)][None]

    def shifted(value, by, axis):
        return pltpu.roll(value, by % value.shape[axis], axis)

    window = pl.ds(row0, C + 2 * HALO)
    inner = pl.ds(row0 + HALO, C)
    column = lax.broadcasted_iota(jnp.int32, (C, NX), 1)
    arrived(edge.at[0], re.at[0], valid=s > 0)
    arrived(edge.at[1], re.at[1], valid=s + 1 < S)

    @pl.when(s == 0)
    def _():
        edge[0] = jnp.zeros((C, NX), jnp.float32)

    @pl.when(s + 1 == S)
    def _():
        edge[1] = jnp.zeros((C, NX), jnp.float32)

    wide = k_ref[4, zi, window]
    middle = wide[HALO : HALO + C]
    lower = jnp.where(zi == 0, edge[0], k_ref[4, jnp.maximum(zi - 1, 0), inner])
    upper = jnp.where(zi == zl - 1, edge[1], k_ref[4, jnp.minimum(zi + 1, zl - 1), inner])
    coupling = k_ref[0, zi, inner]
    adz = coupling * k_ref[1, zi, inner]
    ady = coupling * k_ref[2, zi, inner]
    adx = coupling * k_ref[3, zi, inner]
    summed = (coupling - adz) * upper + (coupling + adz) * lower
    summed += (coupling - ady) * shifted(wide, -1, 0)[HALO : HALO + C]
    summed += (coupling + ady) * shifted(wide, 1, 0)[HALO : HALO + C]
    summed += (coupling - adx) * jnp.where(column == NX - 1, 0.0, shifted(middle, -1, 1))
    summed += (coupling + adx) * jnp.where(column == 0, 0.0, shifted(middle, 1, 1))
    start = summed - 6.0 * coupling * middle

    for d in range(1, T):
        arrived(times.at[lax.rem(t + T - d, T)], r1.at[d])

    for block in range(C // 8):
        rows = slice(block * 8, block * 8 + 8)
        values = [times[m, rows] + start[rows] for m in range(T)]
        for u in range(U):
            for p in range(2):
                total = values[0] * float(forward[u, p, 0])
                for m in range(1, T):
                    total = total + values[m] * float(forward[u, p, m])
                fields[u, p, rows] = total

    z = s * zl + zi
    for step in range(U):
        u = lax.rem(unit + step, U)
        for o in range(q):
            b = (t % per_plane) * q + o
            for kind in range(3):
                to = b + (0, -1, 1)[kind]
                valid = (None, to >= 0, to < bands)[kind]
                safe = jnp.clip(to, 0, bands - 1)
                first, count, land = (
                    (o * R, R, HALO),
                    (o * R, HALO, HALO + R),
                    (o * R + R - HALO, HALO, 0),
                )[kind]
                send(
                    fields.at[u, :, pl.ds(first, count)],
                    src.at[:, z, pl.ds(land, count)],
                    s2.at[step, o, kind],
                    r2.at[z, kind],
                    u * 2 + safe % 2,
                    safe // 2,
                    valid=valid,
                )

    for d in range(S):
        arrived(kbuf.at[:, pl.ds(lax.rem(s + S - d, S) * zl, zl)], rk.at[d])
    angles = [2.0 * math.pi * u / U / 2 for u in range(U)]
    shift_re1 = by_index(unit, [rho * math.cos(a) for a in angles])
    shift_im1 = by_index(unit, [0.0] + [rho * math.sin(a) for a in angles[1:]])
    shift_re2 = by_index(unit, [-rho] + [rho * math.cos(a) for a in angles[1:]])
    wide_column = lax.broadcasted_iota(jnp.int32, (RH, NX), 1)

    @pl.loop(0, NZ)
    def _(z):
        c = kbuf[0, z]
        az = c * kbuf[1, z]
        ay = c * kbuf[2, z]
        ax = c * kbuf[3, z]
        zero = jnp.zeros_like(c)
        coef[0, z] = jnp.where(z == NZ - 1, zero, c - az)
        coef[1, z] = jnp.where(z == 0, zero, c + az)
        coef[2, z] = c - ay
        coef[3, z] = c + ay
        coef[4, z] = jnp.where(wide_column == NX - 1, zero, c - ax)
        coef[5, z] = jnp.where(wide_column == 0, zero, c + ax)
        diag1 = 1.0 + 6.0 * c - shift_re1
        diag2 = 1.0 + 6.0 * c - shift_re2
        im2 = shift_im1 * shift_im1
        modulus1 = diag1 * diag1 + im2
        modulus2 = diag2 * diag2 + im2
        pq[0, z] = diag1 / modulus1
        pq[1, z] = diag2 / modulus2
        pq[2, z] = shift_im1 / modulus1

    @pl.when(band == 0)
    def _():
        src[:, :, :HALO] = jnp.zeros((2, NZ, HALO, NX), jnp.float32)
        last[:, :HALO] = jnp.zeros((NZ, HALO, NX), jnp.float32)
        whalo[0] = jnp.zeros((2, NZ, HALO, NX), jnp.float32)

    @pl.when(band == bands - 1)
    def _():
        src[:, :, HALO + R :] = jnp.zeros((2, NZ, HALO, NX), jnp.float32)
        last[:, HALO + R :] = jnp.zeros((NZ, HALO, NX), jnp.float32)
        whalo[1] = jnp.zeros((2, NZ, HALO, NX), jnp.float32)

    for z in range(NZ):
        arrived(src.at[:, z, pl.ds(HALO, R)], r2.at[z, 0])
        arrived(src.at[:, z, pl.ds(HALO + R, HALO)], r2.at[z, 1], valid=band < bands - 1)
        arrived(src.at[:, z, pl.ds(0, HALO)], r2.at[z, 2], valid=band > 0)

    def scale(z, re_part, im_part, target):
        p1, p2, im = pq[0, z], pq[1, z], pq[2, z]
        target[0, z] = re_part * p1 + im_part * im
        target[1, z] = im_part * p2 - re_part * im

    def sweep(old, new):
        @pl.loop(0, NZ)
        def _(z):
            up = jnp.minimum(z + 1, NZ - 1)
            down = jnp.maximum(z - 1, 0)
            sums = []
            for p in range(2):
                here = old[p, z]
                total = src[p, z] + coef[0, z] * old[p, up] + coef[1, z] * old[p, down]
                total += coef[2, z] * shifted(here, -1, 0) + coef[3, z] * shifted(here, 1, 0)
                total += coef[4, z] * shifted(here, -1, 1) + coef[5, z] * shifted(here, 1, 1)
                sums.append(total)
            scale(z, sums[0], sums[1], new)

    @pl.loop(0, NZ)
    def _(z):
        scale(z, src[0, z], src[1, z], wa)

    @pl.loop(0, SWEEPS // 2)
    def _(i):
        sweep(wa, wb)
        sweep(wb, wa)

    below = jnp.maximum(band - 1, 0)
    above = jnp.minimum(band + 1, bands - 1)
    send(
        wa.at[:, :, pl.ds(HALO + R - HALO, HALO)],
        whalo.at[0],
        sw.at[0],
        rw.at[0],
        unit * 2 + above % 2,
        above // 2,
        valid=band < bands - 1,
        maybe_self=False,
    )
    send(
        wa.at[:, :, pl.ds(HALO, HALO)],
        whalo.at[1],
        sw.at[1],
        rw.at[1],
        unit * 2 + below % 2,
        below // 2,
        valid=band > 0,
        maybe_self=False,
    )
    weight_re = by_index(unit, [float(inverse[u, 0, T - 1]) for u in range(U)])
    weight_im = by_index(unit, [float(inverse[u, 1, T - 1]) for u in range(U)])

    @pl.loop(0, NZ)
    def _(z):
        part[z] = weight_re * wa[0, z, HALO : HALO + R] + weight_im * wa[1, z, HALO : HALO + R]

    for d in range(1, U):
        u = lax.rem(unit + d, U)
        send(
            part.at[pl.ds(u * planes, planes)],
            gathered.at[unit],
            ss.at[d],
            rs.at[d],
            u * 2 + core,
            s,
            maybe_self=False,
        )
    gathered[pl.ds(unit, 1)] = part[pl.ds(unit * planes, planes)][None]
    for d in range(1, U):
        arrived(gathered.at[lax.rem(unit + U - d, U)], rs.at[d])
    total = gathered[0]
    for u in range(1, U):
        total = total + gathered[u]
    reduced[...] = total * rho
    mine = pl.ds(unit * planes, planes)
    for d in range(U):
        u = lax.rem(unit + d, U)
        for kind in range(3):
            to = band + (0, -1, 1)[kind]
            valid = (None, to >= 0, to < bands)[kind]
            safe = jnp.clip(to, 0, bands - 1)
            first, count, land = ((0, R, HALO), (0, HALO, HALO + R), (R - HALO, HALO, 0))[kind]
            if kind == 0 and d == 0:
                last[mine, HALO : HALO + R] = reduced[...]
                continue
            send(
                reduced.at[:, pl.ds(first, count)],
                last.at[mine, pl.ds(land, count)],
                sg.at[d, kind],
                rg.at[d, kind],
                u * 2 + safe % 2,
                safe // 2,
                valid=valid,
                maybe_self=False,
            )
    arrived(whalo.at[0], rw.at[0], valid=band > 0)
    arrived(whalo.at[1], rw.at[1], valid=band < bands - 1)
    sent_before = list(sent)
    sent.clear()
    for finish in sent_before:
        finish()
    wa[:, :, :HALO] = whalo[0]
    wa[:, :, HALO + R :] = whalo[1]
    for d in range(U):
        theirs = pl.ds(lax.rem(unit + U - d, U) * planes, planes)
        if d:
            arrived(last.at[theirs, pl.ds(HALO, R)], rg.at[d, 0])
        arrived(last.at[theirs, pl.ds(HALO + R, HALO)], rg.at[d, 1], valid=band < bands - 1)
        arrived(last.at[theirs, pl.ds(0, HALO)], rg.at[d, 2], valid=band > 0)

    @pl.loop(0, NZ)
    def _(z):
        src[0, z] = src[0, z] - last[z]
        src[1, z] = src[1, z] - jnp.where(unit == 0, last[z], jnp.zeros_like(last[z]))

    @pl.loop(0, SWEEPS // 2)
    def _(i):
        sweep(wa, wb)
        sweep(wb, wa)

    sweep(wa, wb)

    for step in range(NZ):
        z = lax.rem(unit * planes + step, NZ)
        at = (z % zl) * per_plane + (band * R) // C
        offset = pl.multiple_of((band * R) % C, 8)
        send(
            wb.at[:, z, pl.ds(HALO, R)],
            back.at[unit, :, pl.ds(offset, R)],
            s3.at[step],
            r3.at[unit, lax.rem(band, q)],
            at,
            z // zl,
        )
    for u in range(U):
        for o in range(q):
            arrived(back.at[u, :, pl.ds(o * R, R)], r3.at[u, o])
    for block in range(C // 8):
        rows = slice(block * 8, block * 8 + 8)
        values = [back[u, p, rows] for u in range(U) for p in range(2)]
        begin = middle[rows]
        for m in range(T):
            total = begin
            for at in range(T):
                total = total + values[at] * float(inverse[at // 2, at % 2, m] / gamma[m])
            states[m, rows] = total
    for d in range(1, T):
        tt = lax.rem(t + d, T)
        send(
            states.at[tt],
            out_ref.at[pl.ds(pl.multiple_of(t * C, 8), C)],
            s4.at[d],
            r4.at[d],
            tt,
            s,
            maybe_self=False,
        )
    out_ref[pl.ds(pl.multiple_of(t * C, 8), C)] = states[pl.ds(t, 1)][0]
    for d in range(1, T):
        tt = lax.rem(t + T - d, T)
        arrived(out_ref.at[pl.ds(pl.multiple_of(tt * C, 8), C)], r4.at[d])
    for finish in sent:
        finish()


def body(forcing, initial, coupling, velocity):
    local_steps, zl, NY, NX = forcing.shape
    T = lax.axis_size("tm")
    S = lax.axis_size("space")
    U = T // 2
    NZ = zl * S
    C = zl * NY // T
    bands = 2 * S
    R = NY // bands
    RH = R + 2 * HALO
    q = C // R
    planes = NZ // U
    assert local_steps == 1 and SWEEPS <= HALO <= R and ITERS == 2
    assert C % R == 0 and NY % C == 0 and NZ % U == 0
    stacked = jnp.concatenate([coupling[None], velocity, initial[None]], axis=0)
    stacked = jnp.pad(stacked, ((0, 0), (0, 0), (HALO, HALO), (0, 0)))
    f32 = jnp.float32
    dma = pltpu.SemaphoreType.DMA
    out = pl.pallas_call(
        lambda *refs: kernel((T, S, NY, NX, zl), *refs),
        out_shape=jax.ShapeDtypeStruct((zl * NY, NX), f32),
        in_specs=[pl.BlockSpec(memory_space=pltpu.VMEM)] * 2,
        out_specs=pl.BlockSpec(memory_space=pltpu.VMEM),
        scratch_shapes=[
            pltpu.VMEM((T, C, NX), f32),
            pltpu.VMEM((U, 2, C, NX), f32),
            pltpu.VMEM((2, C, NX), f32),
            pltpu.VMEM((4, NZ, RH, NX), f32),
            pltpu.VMEM((6, NZ, RH, NX), f32),
            pltpu.VMEM((3, NZ, RH, NX), f32),
            pltpu.VMEM((2, NZ, RH, NX), f32),
            pltpu.VMEM((2, NZ, RH, NX), f32),
            pltpu.VMEM((2, NZ, RH, NX), f32),
            pltpu.VMEM((2, 2, NZ, HALO, NX), f32),
            pltpu.VMEM((NZ, R, NX), f32),
            pltpu.VMEM((U, planes, R, NX), f32),
            pltpu.VMEM((planes, R, NX), f32),
            pltpu.VMEM((NZ, RH, NX), f32),
            pltpu.VMEM((U, 2, C, NX), f32),
            pltpu.VMEM((T, C, NX), f32),
            dma((T,)),
            dma((T,)),
            dma((U, q, 3)),
            dma((NZ, 3)),
            dma((S,)),
            dma((S,)),
            dma((2,)),
            dma((2,)),
            dma((2,)),
            dma((2,)),
            dma((U,)),
            dma((U,)),
            dma((U, 3)),
            dma((U, 3)),
            dma((NZ,)),
            dma((U, q)),
            dma((T,)),
            dma((T,)),
        ],
        compiler_params=pltpu.CompilerParams(
            has_side_effects=True, vmem_limit_bytes=48 * 1024 * 1024
        ),
    )(forcing.reshape(zl * NY, NX), stacked)
    return out.reshape(forcing.shape)


def solution(mesh):
    return jax.shard_map(
        body,
        mesh=mesh,
        in_specs=(
            P("tm", "space", None, None),
            P("space", None, None),
            P("space", None, None),
            P(None, "space", None, None),
        ),
        out_specs=P("tm", "space", None, None),
        check_vma=False,
    )
```

time: 319 us -> 69 us (0.22)
  waiting for transfers between devices: 113 us -> 0 us
  blocking collectives: 111 us -> 0 us
  Pallas kernels: 0 us -> 66.2 us
  starting transfers between devices: 61.2 us -> 0 us
  other arithmetic: 23.6 us -> 1.42 us
  local copies, waits for them, and re-layouts: 4.47 us -> 0.71 us
  matrix products: 3.5 us -> 0 us
    all_to_all x7 -> x0, blocking collectives: 111 us -> none  [the longest x2 37 us: body(): lax.all_to_all(solved, 'tm', split_axis=3, concat_axis=1, tiled=True)]
    ppermute x38 -> x0, waiting for transfers between devices: 99.2 us -> none  [the longest x18 78 us: with_halo(): lax.ppermute(lax.slice_in_dim(block, 0, width, axis=dim), axis, backward)]
    pallas_call x0 -> x1, Pallas kernels: none -> 66.2 us  [body(): pl.pallas_call(lambda *refs: kernel((T, S, NY, NX, zl), *refs), out_shape...]
    ppermute x38 -> x0, starting transfers between devices: 57.6 us -> none  [the longest x18 29.6 us: with_halo(): lax.ppermute(lax.slice_in_dim(block, block.shape[dim] - width, None, axis...]
    all_to_all x1 -> x0, waiting for transfers between devices: 14.1 us -> none  [body(): lax.all_to_all(spectrum, 'tm', split_axis=1, concat_axis=3, tiled=True)]
    add x18 -> x0, other arithmetic: 9.67 us -> none  [the longest x16 8.91 us: coupled(): total + (coupling - advect[2]) * extended[..., 1:-1, 1:-1, 2:]]
    concatenate x18 -> x1, other arithmetic: 8.58 us -> 1.42 us  [body(): stacked = jnp.concatenate([coupling[None], velocity, initial[None]], axis=0)]
    all_to_all x1 -> x0, starting transfers between devices: 3.57 us -> none  [body(): lax.all_to_all(spectrum, 'tm', split_axis=1, concat_axis=3, tiled=True)]
  transfers between devices with their start and end apart: 39 -> 0, of which waited for: 36 -> 0; matrix products, arithmetic and copies ran while one was open for 1% -> 0% of each run, Pallas kernels for 0% -> 0%
where the time goes in v1:
time: 69 us; the launch traced here: 68.4 us
  Pallas kernels  66.2 us (96%)
  other arithmetic  1.42 us (2%)
  local copies, waits for them, and re-layouts  0.71 us (1%)
    pallas_call x1, Pallas kernels, body(): pl.pallas_call(lambda *refs: kernel((T, S, NY, NX, zl), *refs), out_shape...  66.2 us
    concatenate x1, other arithmetic, body(): stacked = jnp.concatenate([coupling[None], velocity, initial[None]], axis=0)  1.42 us

profile of v1, /device:TPU:0, one launch (start us, length us, event | category | flops | bytes accessed | tf_op | source)
XLA Modules:
  0.0 68.4 jit_solution(11310901033811772432)
XLA Ops:
  0.0 0.0 copy-start
  0.0 1.4 %select_maximum_fusion.refs_1_ = f32[5,4,144,128]{3,2,1,0:T(8,128)S(1)} fusion(f32[1,4,128,128]{3,2,1,0:T(8,128)} %bitcast.6, f32[3,4,128,128]{3,2,1,0:T(8,128)} %param.7, f32[1,4,128,128]{3,2,1,0:T(8,128)} %bitcast.7), kind=kLoop, calls=%fused_computation.2 | loop fusion | flops 2949120 | bytes 2785280 | tf_op jit(solution)/shard_map/concatenate | solution.py:510
  1.4 0.0 copy-done
  1.4 66.2 %shard_map.46 = f32[512,128]{1,0:T(8,128)S(1)} custom-call(f32[512,128]{1,0:T(8,128)S(1)} %bitcast.5, f32[5,4,144,128]{3,2,1,0:T(8,128)S(1)} %select_maximum_fusion.refs_1_), custom_call_target="tpu_custom_call" | custom-call | tf_op jit(solution)/shard_map/pallas_call | solution.py:514
  67.7 0.7 %copy.6 = f32[1,4,128,128]{3,2,1,0:T(8,128)} copy(f32[1,4,128,128]{3,2,1,0:T(8,128)S(1)} %bitcast.4) | data formatting | bytes 524288
Async XLA Ops:
  0.0 1.4 %copy-start = (f32[1,4,128,128]{3,2,1,0:T(8,128)S(1)}, f32[1,4,128,128]{3,2,1,0:T(8,128)}, u32[]{:S(2)}) copy-start(f32[1,4,128,128]{3,2,1,0:T(8,128)} %param.4) | copy-start | bytes 786436

commit v2 on v1

--- a/solution.py
+++ b/solution.py
@@ -99,7 +99,6 @@
     R = NY // bands
     RH = R + 2 * HALO
     q = C // R
-    per_plane = NY // C
     planes = NZ // U
     rho = wrap_alpha ** (1.0 / T)
     forward = forward_table(T)
@@ -109,11 +108,21 @@
 
     t = lax.axis_index("tm")
     s = lax.axis_index("space")
-    unit = t // 2
-    core = t % 2
-    band = s * 2 + core
-    zi = t // per_plane
-    row0 = pl.multiple_of((t % per_plane) * C, 8)
+    group = t // zl
+    zi = t % zl
+    unit = (zi * S + s) // q
+    band = group * q + (zi * S + s) % q
+    row0 = pl.multiple_of(group * C, 8)
+
+    def place(u, b):
+        at = u * q + b % q
+        return (b // q) * zl + at // S, at % S
+
+    def chunk(tt):
+        start = (tt % zl) * NY + (tt // zl) * C
+        return pl.ds(pl.multiple_of(start, 8), C)
+
+    far_first = sorted(range(1, T), key=lambda d: -min(d, T - d))
 
     def device(tt, ts):
         return {"tm": tt, "space": ts}
@@ -169,10 +178,10 @@
             def _():
                 pltpu.make_async_copy(target, target, rsem).wait()
 
-    for d in range(1, T):
+    for d in far_first:
         tt = lax.rem(t + d, T)
         send(
-            f_ref.at[pl.ds(pl.multiple_of(tt * C, 8), C)],
+            f_ref.at[chunk(tt)],
             times.at[t],
             s1.at[d],
             r1.at[d],
@@ -202,14 +211,14 @@
     )
     for d in range(S):
         ts = lax.rem(s + d, S)
-        rows = pl.ds(pl.multiple_of((ts * 2 + core) * R, 8), RH)
+        rows = pl.ds(pl.multiple_of((group * q + (zi * S + ts) % q) * R, 8), RH)
         source = k_ref.at[pl.ds(0, 4), :, rows]
         target = kbuf.at[:, pl.ds(s * zl, zl)]
         if d:
             send(source, target, sk.at[d], rk.at[d], t, ts, maybe_self=False)
         else:
             pltpu.make_async_copy(source, target, rk.at[0]).start()
-    times[pl.ds(t, 1)] = f_ref[pl.ds(pl.multiple_of(t * C, 8), C)][None]
+    times[pl.ds(t, 1)] = f_ref[chunk(t)][None]
 
     def shifted(value, by, axis):
         return pltpu.roll(value, by % value.shape[axis], axis)
@@ -260,7 +269,7 @@
     for step in range(U):
         u = lax.rem(unit + step, U)
         for o in range(q):
-            b = (t % per_plane) * q + o
+            b = group * q + o
             for kind in range(3):
                 to = b + (0, -1, 1)[kind]
                 valid = (None, to >= 0, to < bands)[kind]
@@ -270,13 +279,14 @@
                     (o * R, HALO, HALO + R),
                     (o * R + R - HALO, HALO, 0),
                 )[kind]
+                to_t, to_s = place(u, safe)
                 send(
                     fields.at[u, :, pl.ds(first, count)],
                     src.at[:, z, pl.ds(land, count)],
                     s2.at[step, o, kind],
                     r2.at[z, kind],
-                    u * 2 + safe % 2,
-                    safe // 2,
+                    to_t,
+                    to_s,
                     valid=valid,
                 )
 
@@ -332,19 +342,23 @@
         target[0, z] = re_part * p1 + im_part * im
         target[1, z] = im_part * p2 - re_part * im
 
+    together = math.gcd(NZ, 8)
+
     def sweep(old, new):
-        @pl.loop(0, NZ)
-        def _(z):
-            up = jnp.minimum(z + 1, NZ - 1)
-            down = jnp.maximum(z - 1, 0)
-            sums = []
-            for p in range(2):
-                here = old[p, z]
-                total = src[p, z] + coef[0, z] * old[p, up] + coef[1, z] * old[p, down]
-                total += coef[2, z] * shifted(here, -1, 0) + coef[3, z] * shifted(here, 1, 0)
-                total += coef[4, z] * shifted(here, -1, 1) + coef[5, z] * shifted(here, 1, 1)
-                sums.append(total)
-            scale(z, sums[0], sums[1], new)
+        @pl.loop(0, NZ // together)
+        def _(trip):
+            for o in range(together):
+                z = trip * together + o
+                up = jnp.minimum(z + 1, NZ - 1) if o == together - 1 else z + 1
+                down = jnp.maximum(z - 1, 0) if o == 0 else z - 1
+                sums = []
+                for p in range(2):
+                    here = old[p, z]
+                    total = src[p, z] + coef[0, z] * old[p, up] + coef[1, z] * old[p, down]
+                    total += coef[2, z] * shifted(here, -1, 0) + coef[3, z] * shifted(here, 1, 0)
+                    total += coef[4, z] * shifted(here, -1, 1) + coef[5, z] * shifted(here, 1, 1)
+                    sums.append(total)
+                scale(z, sums[0], sums[1], new)
 
     @pl.loop(0, NZ)
     def _(z):
@@ -362,8 +376,7 @@
         whalo.at[0],
         sw.at[0],
         rw.at[0],
-        unit * 2 + above % 2,
-        above // 2,
+        *place(unit, above),
         valid=band < bands - 1,
         maybe_self=False,
     )
@@ -372,8 +385,7 @@
         whalo.at[1],
         sw.at[1],
         rw.at[1],
-        unit * 2 + below % 2,
-        below // 2,
+        *place(unit, below),
         valid=band > 0,
         maybe_self=False,
     )
@@ -391,8 +403,7 @@
             gathered.at[unit],
             ss.at[d],
             rs.at[d],
-            u * 2 + core,
-            s,
+            *place(u, band),
             maybe_self=False,
         )
     gathered[pl.ds(unit, 1)] = part[pl.ds(unit * planes, planes)][None]
@@ -418,8 +429,7 @@
                 last.at[mine, pl.ds(land, count)],
                 sg.at[d, kind],
                 rg.at[d, kind],
-                u * 2 + safe % 2,
-                safe // 2,
+                *place(u, safe),
                 valid=valid,
                 maybe_self=False,
             )
@@ -452,8 +462,8 @@
 
     for step in range(NZ):
         z = lax.rem(unit * planes + step, NZ)
-        at = (z % zl) * per_plane + (band * R) // C
-        offset = pl.multiple_of((band * R) % C, 8)
+        at = group * zl + z % zl
+        offset = pl.multiple_of((band % q) * R, 8)
         send(
             wb.at[:, z, pl.ds(HALO, R)],
             back.at[unit, :, pl.ds(offset, R)],
@@ -474,21 +484,21 @@
             for at in range(T):
                 total = total + values[at] * float(inverse[at // 2, at % 2, m] / gamma[m])
             states[m, rows] = total
-    for d in range(1, T):
+    for d in far_first:
         tt = lax.rem(t + d, T)
         send(
             states.at[tt],
-            out_ref.at[pl.ds(pl.multiple_of(t * C, 8), C)],
+            out_ref.at[chunk(t)],
             s4.at[d],
             r4.at[d],
             tt,
             s,
             maybe_self=False,
         )
-    out_ref[pl.ds(pl.multiple_of(t * C, 8), C)] = states[pl.ds(t, 1)][0]
+    out_ref[chunk(t)] = states[pl.ds(t, 1)][0]
     for d in range(1, T):
         tt = lax.rem(t + T - d, T)
-        arrived(out_ref.at[pl.ds(pl.multiple_of(tt * C, 8), C)], r4.at[d])
+        arrived(out_ref.at[chunk(tt)], r4.at[d])
     for finish in sent:
         finish()
 

time: 69 us -> 53.5 us (0.78)
  Pallas kernels: 66.2 us -> 51.2 us
    pallas_call x1, Pallas kernels: 66.2 us -> 51.2 us  [body(): pl.pallas_call(lambda *refs: kernel((T, S, NY, NX, zl), *refs), out_shape...]
where the time goes in v2:
time: 53.5 us; the launch traced here: 53.3 us
  Pallas kernels  51.2 us (96%)
  other arithmetic  1.42 us (3%)
  local copies, waits for them, and re-layouts  0.71 us (1%)
    pallas_call x1, Pallas kernels, body(): pl.pallas_call(lambda *refs: kernel((T, S, NY, NX, zl), *refs), out_shape...  51.2 us
    concatenate x1, other arithmetic, body(): stacked = jnp.concatenate([coupling[None], velocity, initial[None]], axis=0)  1.42 us

profile of v2, /device:TPU:0, one launch (start us, length us, event | category | flops | bytes accessed | tf_op | source)
XLA Modules:
  0.0 53.3 jit_solution(418027279057320970)
XLA Ops:
  0.0 0.0 copy-start
  0.0 1.4 %select_maximum_fusion.refs_1_ = f32[5,4,144,128]{3,2,1,0:T(8,128)S(1)} fusion(f32[1,4,128,128]{3,2,1,0:T(8,128)} %bitcast.6, f32[3,4,128,128]{3,2,1,0:T(8,128)} %param.7, f32[1,4,128,128]{3,2,1,0:T(8,128)} %bitcast.7), kind=kLoop, calls=%fused_computation.2 | loop fusion | flops 2949120 | bytes 2785280 | tf_op jit(solution)/shard_map/concatenate | solution.py:520
  1.4 0.0 copy-done
  1.4 51.2 %shard_map.46 = f32[512,128]{1,0:T(8,128)S(1)} custom-call(f32[512,128]{1,0:T(8,128)S(1)} %bitcast.5, f32[5,4,144,128]{3,2,1,0:T(8,128)S(1)} %select_maximum_fusion.refs_1_), custom_call_target="tpu_custom_call" | custom-call | tf_op jit(solution)/shard_map/pallas_call | solution.py:524
  52.6 0.7 %copy.6 = f32[1,4,128,128]{3,2,1,0:T(8,128)} copy(f32[1,4,128,128]{3,2,1,0:T(8,128)S(1)} %bitcast.4) | data formatting | bytes 524288
Async XLA Ops:
  0.0 1.4 %copy-start = (f32[1,4,128,128]{3,2,1,0:T(8,128)S(1)}, f32[1,4,128,128]{3,2,1,0:T(8,128)}, u32[]{:S(2)}) copy-start(f32[1,4,128,128]{3,2,1,0:T(8,128)} %param.4) | copy-start | bytes 786436

commit v3 on v2

--- a/solution.py
+++ b/solution.py
@@ -137,6 +137,12 @@
             device_id_type=pl.DeviceIdType.MESH,
         )
 
+    barrier = pltpu.get_barrier_semaphore()
+    for d in range(1, T):
+        pl.semaphore_signal(barrier, inc=1, device_id=device(lax.rem(t + d, T), s), device_id_type=pl.DeviceIdType.MESH)
+    for d in range(1, S):
+        pl.semaphore_signal(barrier, inc=1, device_id=device(t, lax.rem(s + d, S)), device_id_type=pl.DeviceIdType.MESH)
+    pl.semaphore_wait(barrier, T + S - 2)
     sent = []
 
     def send(source, target, ssem, rsem, tt, ts, valid=None, maybe_self=True):
@@ -209,16 +215,43 @@
         valid=s > 0,
         maybe_self=False,
     )
-    for d in range(S):
+    for d in range(1, S):
         ts = lax.rem(s + d, S)
         rows = pl.ds(pl.multiple_of((group * q + (zi * S + ts) % q) * R, 8), RH)
         source = k_ref.at[pl.ds(0, 4), :, rows]
         target = kbuf.at[:, pl.ds(s * zl, zl)]
-        if d:
-            send(source, target, sk.at[d], rk.at[d], t, ts, maybe_self=False)
-        else:
-            pltpu.make_async_copy(source, target, rk.at[0]).start()
+        send(source, target, sk.at[d], rk.at[d], t, ts, maybe_self=False)
     times[pl.ds(t, 1)] = f_ref[chunk(t)][None]
+
+    angles = [2.0 * math.pi * u / U / 2 for u in range(U)]
+    shift_re1 = by_index(unit, [rho * math.cos(a) for a in angles])
+    shift_im1 = by_index(unit, [0.0] + [rho * math.sin(a) for a in angles[1:]])
+    shift_re2 = by_index(unit, [-rho] + [rho * math.cos(a) for a in angles[1:]])
+    wide_column = lax.broadcasted_iota(jnp.int32, (RH, NX), 1)
+
+    def prepare(z, c, vz, vy, vx):
+        az = c * vz
+        ay = c * vy
+        ax = c * vx
+        zero = jnp.zeros_like(c)
+        coef[0, z] = jnp.where(z == NZ - 1, zero, c - az)
+        coef[1, z] = jnp.where(z == 0, zero, c + az)
+        coef[2, z] = c - ay
+        coef[3, z] = c + ay
+        coef[4, z] = jnp.where(wide_column == NX - 1, zero, c - ax)
+        coef[5, z] = jnp.where(wide_column == 0, zero, c + ax)
+        diag1 = 1.0 + 6.0 * c - shift_re1
+        diag2 = 1.0 + 6.0 * c - shift_re2
+        im2 = shift_im1 * shift_im1
+        modulus1 = diag1 * diag1 + im2
+        modulus2 = diag2 * diag2 + im2
+        pq[0, z] = diag1 / modulus1
+        pq[1, z] = diag2 / modulus2
+        pq[2, z] = shift_im1 / modulus1
+
+    band_rows = pl.ds(pl.multiple_of(band * R, 8), RH)
+    for o in range(zl):
+        prepare(s * zl + o, *[k_ref[m, o, band_rows] for m in range(4)])
 
     def shifted(value, by, axis):
         return pltpu.roll(value, by % value.shape[axis], axis)
@@ -290,35 +323,11 @@
                     valid=valid,
                 )
 
-    for d in range(S):
-        arrived(kbuf.at[:, pl.ds(lax.rem(s + S - d, S) * zl, zl)], rk.at[d])
-    angles = [2.0 * math.pi * u / U / 2 for u in range(U)]
-    shift_re1 = by_index(unit, [rho * math.cos(a) for a in angles])
-    shift_im1 = by_index(unit, [0.0] + [rho * math.sin(a) for a in angles[1:]])
-    shift_re2 = by_index(unit, [-rho] + [rho * math.cos(a) for a in angles[1:]])
-    wide_column = lax.broadcasted_iota(jnp.int32, (RH, NX), 1)
-
-    @pl.loop(0, NZ)
-    def _(z):
-        c = kbuf[0, z]
-        az = c * kbuf[1, z]
-        ay = c * kbuf[2, z]
-        ax = c * kbuf[3, z]
-        zero = jnp.zeros_like(c)
-        coef[0, z] = jnp.where(z == NZ - 1, zero, c - az)
-        coef[1, z] = jnp.where(z == 0, zero, c + az)
-        coef[2, z] = c - ay
-        coef[3, z] = c + ay
-        coef[4, z] = jnp.where(wide_column == NX - 1, zero, c - ax)
-        coef[5, z] = jnp.where(wide_column == 0, zero, c + ax)
-        diag1 = 1.0 + 6.0 * c - shift_re1
-        diag2 = 1.0 + 6.0 * c - shift_re2
-        im2 = shift_im1 * shift_im1
-        modulus1 = diag1 * diag1 + im2
-        modulus2 = diag2 * diag2 + im2
-        pq[0, z] = diag1 / modulus1
-        pq[1, z] = diag2 / modulus2
-        pq[2, z] = shift_im1 / modulus1
+    for d in range(1, S):
+        theirs = lax.rem(s + S - d, S) * zl
+        arrived(kbuf.at[:, pl.ds(theirs, zl)], rk.at[d])
+        for o in range(zl):
+            prepare(theirs + o, *[kbuf[m, theirs + o] for m in range(4)])
 
     @pl.when(band == 0)
     def _():
@@ -563,7 +572,7 @@
             dma((T,)),
         ],
         compiler_params=pltpu.CompilerParams(
-            has_side_effects=True, vmem_limit_bytes=48 * 1024 * 1024
+            has_side_effects=True, collective_id=0, vmem_limit_bytes=48 * 1024 * 1024
         ),
     )(forcing.reshape(zl * NY, NX), stacked)
     return out.reshape(forcing.shape)

time: 53.5 us -> 49.5 us (0.925)
  Pallas kernels: 51.2 us -> 47.2 us
    pallas_call x1, Pallas kernels: 51.2 us -> 47.2 us  [body(): pl.pallas_call(lambda *refs: kernel((T, S, NY, NX, zl), *refs), out_shape...]
where the time goes in v3:
time: 49.5 us; the launch traced here: 49.4 us
  Pallas kernels  47.2 us (95%)
  other arithmetic  1.42 us (3%)
  local copies, waits for them, and re-layouts  0.71 us (1%)
    pallas_call x1, Pallas kernels, body(): pl.pallas_call(lambda *refs: kernel((T, S, NY, NX, zl), *refs), out_shape...  47.2 us
    concatenate x1, other arithmetic, body(): stacked = jnp.concatenate([coupling[None], velocity, initial[None]], axis=0)  1.42 us

profile of v3, /device:TPU:0, one launch (start us, length us, event | category | flops | bytes accessed | tf_op | source)
XLA Modules:
  0.0 49.4 jit_solution(17420196878297957905)
XLA Ops:
  0.0 0.0 copy-start
  0.0 1.4 %select_maximum_fusion.refs_1_ = f32[5,4,144,128]{3,2,1,0:T(8,128)S(1)} fusion(f32[1,4,128,128]{3,2,1,0:T(8,128)} %bitcast.6, f32[3,4,128,128]{3,2,1,0:T(8,128)} %param.7, f32[1,4,128,128]{3,2,1,0:T(8,128)} %bitcast.7), kind=kLoop, calls=%fused_computation.2 | loop fusion | flops 2949120 | bytes 2785280 | tf_op jit(solution)/shard_map/concatenate | solution.py:529
  1.4 0.0 copy-done
  1.4 47.2 %shard_map.46 = f32[512,128]{1,0:T(8,128)S(1)} custom-call(f32[512,128]{1,0:T(8,128)S(1)} %bitcast.5, f32[5,4,144,128]{3,2,1,0:T(8,128)S(1)} %select_maximum_fusion.refs_1_), custom_call_target="tpu_custom_call" | custom-call | tf_op jit(solution)/shard_map/pallas_call | solution.py:533
  48.7 0.7 %copy.6 = f32[1,4,128,128]{3,2,1,0:T(8,128)} copy(f32[1,4,128,128]{3,2,1,0:T(8,128)S(1)} %bitcast.4) | data formatting | bytes 524288
Async XLA Ops:
  0.0 1.4 %copy-start = (f32[1,4,128,128]{3,2,1,0:T(8,128)S(1)}, f32[1,4,128,128]{3,2,1,0:T(8,128)}, u32[]{:S(2)}) copy-start(f32[1,4,128,128]{3,2,1,0:T(8,128)} %param.4) | copy-start | bytes 786436

commit v4 on v3

--- a/solution.py
+++ b/solution.py
@@ -78,6 +78,8 @@
     r2,
     sk,
     rk,
+    sf,
+    rf,
     se,
     re,
     sw,
@@ -122,7 +124,7 @@
         start = (tt % zl) * NY + (tt // zl) * C
         return pl.ds(pl.multiple_of(start, 8), C)
 
-    far_first = sorted(range(1, T), key=lambda d: -min(d, T - d))
+    ring = range(1, T)
 
     def device(tt, ts):
         return {"tm": tt, "space": ts}
@@ -184,7 +186,7 @@
             def _():
                 pltpu.make_async_copy(target, target, rsem).wait()
 
-    for d in far_first:
+    for d in ring:
         tt = lax.rem(t + d, T)
         send(
             f_ref.at[chunk(tt)],
@@ -215,11 +217,15 @@
         valid=s > 0,
         maybe_self=False,
     )
+    half = zl // 2
+    share = (t % 2) * half
+    rest = half - share
+    partner = t + 1 - 2 * (t % 2)
     for d in range(1, S):
         ts = lax.rem(s + d, S)
         rows = pl.ds(pl.multiple_of((group * q + (zi * S + ts) % q) * R, 8), RH)
-        source = k_ref.at[pl.ds(0, 4), :, rows]
-        target = kbuf.at[:, pl.ds(s * zl, zl)]
+        source = k_ref.at[pl.ds(0, 4), pl.ds(share, half), rows]
+        target = kbuf.at[:, pl.ds(s * zl + share, half)]
         send(source, target, sk.at[d], rk.at[d], t, ts, maybe_self=False)
     times[pl.ds(t, 1)] = f_ref[chunk(t)][None]
 
@@ -325,9 +331,18 @@
 
     for d in range(1, S):
         theirs = lax.rem(s + S - d, S) * zl
-        arrived(kbuf.at[:, pl.ds(theirs, zl)], rk.at[d])
-        for o in range(zl):
-            prepare(theirs + o, *[kbuf[m, theirs + o] for m in range(4)])
+        block = kbuf.at[:, pl.ds(theirs + share, half)]
+        arrived(block, rk.at[d])
+        send(block, block, sf.at[d], rf.at[d], partner, s, maybe_self=False)
+    for d in range(1, S):
+        theirs = lax.rem(s + S - d, S) * zl
+        for o in range(half):
+            at = theirs + share + o
+            prepare(at, *[kbuf[m, at] for m in range(4)])
+        arrived(kbuf.at[:, pl.ds(theirs + rest, half)], rf.at[d])
+        for o in range(half):
+            at = theirs + rest + o
+            prepare(at, *[kbuf[m, at] for m in range(4)])
 
     @pl.when(band == 0)
     def _():
@@ -493,7 +508,7 @@
             for at in range(T):
                 total = total + values[at] * float(inverse[at // 2, at % 2, m] / gamma[m])
             states[m, rows] = total
-    for d in far_first:
+    for d in ring:
         tt = lax.rem(t + d, T)
         send(
             states.at[tt],
@@ -525,6 +540,7 @@
     q = C // R
     planes = NZ // U
     assert local_steps == 1 and SWEEPS <= HALO <= R and ITERS == 2
+    assert S % q == 0 and zl % 2 == 0 and T % 2 == 0
     assert C % R == 0 and NY % C == 0 and NZ % U == 0
     stacked = jnp.concatenate([coupling[None], velocity, initial[None]], axis=0)
     stacked = jnp.pad(stacked, ((0, 0), (0, 0), (HALO, HALO), (0, 0)))
@@ -558,6 +574,8 @@
             dma((NZ, 3)),
             dma((S,)),
             dma((S,)),
+            dma((S,)),
+            dma((S,)),
             dma((2,)),
             dma((2,)),
             dma((2,)),

time: 49.5 us -> 47.3 us (0.956)
  Pallas kernels: 47.2 us -> 44.8 us
    pallas_call x1, Pallas kernels: 47.2 us -> 44.8 us  [body(): pl.pallas_call(lambda *refs: kernel((T, S, NY, NX, zl), *refs), out_shape...]
where the time goes in v4:
time: 47.3 us; the launch traced here: 47 us
  Pallas kernels  44.8 us (95%)
  other arithmetic  1.42 us (3%)
  local copies, waits for them, and re-layouts  0.71 us (2%)
    pallas_call x1, Pallas kernels, body(): pl.pallas_call(lambda *refs: kernel((T, S, NY, NX, zl), *refs), out_shape...  44.8 us
    concatenate x1, other arithmetic, body(): stacked = jnp.concatenate([coupling[None], velocity, initial[None]], axis=0)  1.42 us

profile of v4, /device:TPU:0, one launch (start us, length us, event | category | flops | bytes accessed | tf_op | source)
XLA Modules:
  0.0 47.0 jit_solution(7756467580331032594)
XLA Ops:
  0.0 0.0 copy-start
  0.0 1.4 %select_maximum_fusion.refs_1_ = f32[5,4,144,128]{3,2,1,0:T(8,128)S(1)} fusion(f32[1,4,128,128]{3,2,1,0:T(8,128)} %bitcast.6, f32[3,4,128,128]{3,2,1,0:T(8,128)} %param.7, f32[1,4,128,128]{3,2,1,0:T(8,128)} %bitcast.7), kind=kLoop, calls=%fused_computation.2 | loop fusion | flops 2949120 | bytes 2785280 | tf_op jit(solution)/shard_map/concatenate | solution.py:545
  1.4 0.0 copy-done
  1.4 44.8 %shard_map.46 = f32[512,128]{1,0:T(8,128)S(1)} custom-call(f32[512,128]{1,0:T(8,128)S(1)} %bitcast.5, f32[5,4,144,128]{3,2,1,0:T(8,128)S(1)} %select_maximum_fusion.refs_1_), custom_call_target="tpu_custom_call" | custom-call | tf_op jit(solution)/shard_map/pallas_call | solution.py:549
  46.3 0.7 %copy.6 = f32[1,4,128,128]{3,2,1,0:T(8,128)} copy(f32[1,4,128,128]{3,2,1,0:T(8,128)S(1)} %bitcast.4) | data formatting | bytes 524288
Async XLA Ops:
  0.0 1.4 %copy-start = (f32[1,4,128,128]{3,2,1,0:T(8,128)S(1)}, f32[1,4,128,128]{3,2,1,0:T(8,128)}, u32[]{:S(2)}) copy-start(f32[1,4,128,128]{3,2,1,0:T(8,128)} %param.4) | copy-start | bytes 786436
